TPU v7x, 32 devices: a whole 2x2x4 slice. The times are simulated.
32 devices in a mesh: blk: 16 (over z, y, core), grp: 2 (over x).
Axes of the slice: x: 2, y: 2, z: 4, core: 2. Of those that a mesh axis runs over, the one named last changes fastest.
Arguments:
- layer_one: bfloat16 [1792, 1024], P(('blk', 'grp')), may hold values from -6 to 6
- layer_two: bfloat16 [1792, 1024], P(('blk', 'grp')), may hold values from -6 to 6
- spread: int32 [2], replicated, may hold values from 1024 to 4096
Outputs:
- profiles: float32 [2, 1792], P(None, ('blk', 'grp'))
- alignment: float32 [], replicated
All inputs are finite; a program needn't handle non-finite values.
Results may differ from a plain program's by a relative error of at most 0.0003.
Values may be sent and summed in bfloat16 or wider, within the bound.
A program may use at most 128 MiB of HBM per device.

v0:
```python
import jax
import jax.numpy as jnp
from jax import lax
from jax.sharding import PartitionSpec as P

D = 1024


def kernel_block(rows, sq_rows, cols, scale, offset):
    sq_cols = jnp.sum(cols.astype(jnp.float32) ** 2, axis=1)
    inner = lax.dot_general(
        rows, cols, (((1,), (1,)), ((), ())), preferred_element_type=jnp.float32
    )
    dist = sq_rows[:, None] + sq_cols[None, :] - 2.0 * inner
    return jnp.exp(-dist / (2.0 * scale)) - offset


def shards(layer_one, layer_two, spread):
    scales = spread.astype(jnp.float32)
    offsets = jnp.exp(-D / scales)
    stacked = jnp.stack([layer_one, layer_two])
    paired = lax.all_gather(stacked, "grp", axis=1, tiled=True)
    sq_pair = jnp.sum(paired.astype(jnp.float32) ** 2, axis=2)
    block = lax.all_gather(stacked, "blk", axis=1, tiled=True)
    first = kernel_block(paired[0], sq_pair[0], block[0], scales[0], offsets[0])
    second = kernel_block(paired[1], sq_pair[1], block[1], scales[1], offsets[1])
    first, second = (first, second)
    rows_acc = jnp.stack([jnp.sum(first, axis=1), jnp.sum(second, axis=1)])
    prods = jnp.stack([jnp.sum(first * second), jnp.sum(first * first), jnp.sum(second * second)])
    rows_acc, prods = (rows_acc, prods)
    own_rows = lax.psum_scatter(rows_acc, "grp", scatter_dimension=1, tiled=True)
    total = own_rows.shape[1] * lax.axis_size("blk") * lax.axis_size("grp")
    row_terms = jnp.stack(
        [
            jnp.sum(own_rows[0]),
            jnp.sum(own_rows[1]),
            jnp.sum(own_rows[0] * own_rows[1]),
            jnp.sum(own_rows[0] * own_rows[0]),
            jnp.sum(own_rows[1] * own_rows[1]),
        ]
    )
    prods = lax.psum(prods, ("blk", "grp"))
    row_terms = lax.psum(row_terms, ("blk", "grp"))
    sum_one, sum_two = (row_terms[0], row_terms[1])
    c_cross, c_one, c_two = (row_terms[2], row_terms[3], row_terms[4])
    h_cross = prods[0] - 2.0 * c_cross / total + sum_one * sum_two / (total * total)
    h_one = prods[1] - 2.0 * c_one / total + sum_one * sum_one / (total * total)
    h_two = prods[2] - 2.0 * c_two / total + sum_two * sum_two / (total * total)
    alignment = h_cross / jnp.sqrt(h_one * h_two)
    profiles = jnp.stack(
        [own_rows[0] / jnp.sqrt(c_one / total), own_rows[1] / jnp.sqrt(c_two / total)]
    )
    return (profiles, alignment)


def solution(mesh):
    return jax.shard_map(
        shards,
        mesh=mesh,
        in_specs=(P(("blk", "grp"), None), P(("blk", "grp"), None), P()),
        out_specs=(P(None, ("blk", "grp")), P()),
        check_vma=False,
    )
```

profile of v0, /device:TPU:0, one launch (start us, length us, event | category | flops | bytes accessed | tf_op | source)
XLA Modules:
  0.0 135.6 jit_solution(13423032327136159622)
XLA Ops:
  7.2 0.0 all-gather.2.cloned.1.call-start
  7.2 1.7 %pad_maximum_fusion = bf16[2,56,1024]{2,1,0:T(8,128)(2,1)} fusion(bf16[1,56,1024]{2,1,0:T(8,128)(2,1)} %bitcast.70, bf16[1,56,1024]{2,1,0:T(8,128)(2,1)} %bitcast.71), kind=kLoop, calls=%fused_computation.24 | loop fusion | flops 114688 | bytes 458752 | tf_op jit(solution)/shard_map/stack | solution.py:21
  8.9 0.0 all-gather.2.cloned.1.call-update
  8.9 0.7 convert_element_type.14
  9.6 0.6 fusion.16
  11.5 1.2 dynamic-slice
  13.4 0.7 divide_exponential_fusion
  14.0 0.6 fusion.17
  14.6 9.5 %all_gather.6 = bf16[2,112,1024]{2,1,0:T(8,128)(2,1)S(1)} all-gather(bf16[2,56,1024]{2,1,0:T(8,128)(2,1)} %pad_maximum_fusion), channel_id=1, replica_groups=mesh['blk'=16,'grp'=2] {'grp'}, dimensions={1}, use_global_device_ids=true | all-gather | bytes 688128 | tf_op jit(solution)/shard_map/all_gather | solution.py:22
  24.1 0.2 multiply_reduce_fusion.2
  24.3 36.4 %all-gather.2.cloned.1.call-done = bf16[2,896,1024]{2,1,0:T(8,128)(2,1)} async-done(((bf16[2,56,1024]{2,1,0:T(8,128)(2,1)}), bf16[2,896,1024]{2,1,0:T(8,128)(2,1)}) %all-gather.2.cloned.1.call-update) | async-done | bytes 3670032 | tf_op jit(solution)/shard_map/all_gather | solution.py:24
  60.7 0.0 copy-start
  60.7 3.0 %multiply_reduce_fusion.1 = (f32[896]{0:T(1024)S(1)}, f32[896]{0:T(1024)S(1)}) fusion(bf16[2,896,1024]{2,1,0:T(8,128)(2,1)} %all-gather.2.cloned.1.call-done), kind=kLoop, calls=%fused_computation.1 | loop fusion | flops 5503232 | bytes 3677184 | tf_op jit(solution)/shard_map/reduce_sum | solution.py:10
  63.7 0.2 copy-done
  63.8 1.4 %fusion.10 = f32[112,896]{1,0:T(8,128)S(1)} fusion(bf16[2,896,1024]{2,1,0:T(8,128)(2,1)S(1)} %copy-done, bf16[2,112,1024]{2,1,0:T(8,128)(2,1)S(1)} %all_gather.6, f32[]{:T(128)} %bitcast.12, f32[]{:T(128)} %bitcast.11, f32[896]{0:T(1024)S(1)} %get-tuple-element.3, f32[112]{0:T(128)S(1)} %get-tuple-element.18), kind=kOutput, calls=%fused_computation.14 | convolution fusion | flops 206123008 | bytes 2470408 | tf_op jit(solution)/shard_map/dot_general | solution.py:11
  65.2 2.1 %multiply_reduce_fusion.5 = (f32[]{:T(128)}, f32[]{:T(128)}, f32[112]{0:T(128)S(1)}, f32[]{:T(128)}, f32[112]{0:T(128)S(1)}) fusion(f32[112,896]{1,0:T(8,128)S(1)} %fusion.10, f32[]{:T(128)} %bitcast.6, f32[]{:T(128)} %bitcast.5, bf16[2,896,1024]{2,1,0:T(8,128)(2,1)S(1)} %copy-done, bf16[2,112,1024]{2,1,0:T(8,128)(2,1)S(1)} %all_gather.6, ...), kind=kOutput, calls=%fused_computation.21 | convolution fusion | flops 206925600 | bytes 2471316 | tf_op jit(solution)/shard_map/dot_general | solution.py:11
  67.4 4.9 %all-reduce = f32[2,112]{1,0:T(2,128)S(1)} all-reduce(f32[2,112]{1,0:T(2,128)S(1)} %pad_maximum_fusion.1), channel_id=2, replica_groups=mesh['blk'=16,'grp'=2] {'grp'}, use_global_device_ids=true, to_apply=%region_5.0.clone | all-reduce | flops 224 | bytes 1792
  72.3 0.1 constant_dynamic-slice_fusion
  72.4 0.7 multiply_reduce_fusion.6
  73.0 2.0 %pad_maximum_fusion.3 = f32[3]{0:T(128)S(1)} fusion(f32[1]{0:T(128)} %bitcast.23, f32[1]{0:T(128)} %bitcast.22, f32[1]{0:T(128)} %bitcast.21), kind=kLoop, calls=%fused_computation.27 | loop fusion | flops 6 | bytes 24 | tf_op jit(solution)/shard_map/stack | solution.py:29
  75.0 3.2 %stack.64 = f32[5]{0:T(128)S(1)} concatenate(f32[1]{0:T(128)} %bitcast.14, f32[1]{0:T(128)} %bitcast.15, f32[1]{0:T(128)} %bitcast.16, f32[1]{0:T(128)} %bitcast.17, f32[1]{0:T(128)} %bitcast.18), dimensions={0} | concatenate | bytes 40 | tf_op jit(solution)/shard_map/stack | solution.py:33
  78.2 39.4 %all-reduce.1 = (f32[5]{0:T(128)S(1)}, f32[3]{0:T(128)S(1)}) all-reduce(f32[5]{0:T(128)S(1)} %stack.64, f32[3]{0:T(128)S(1)} %pad_maximum_fusion.3), channel_id=1, replica_groups=mesh['blk'=16,'grp'=2] {'blk','grp'}, use_global_device_ids=true, to_apply=%region_11.0 | all-reduce | flops 8 | bytes 64 | tf_op jit(solution)/shard_map/psum | solution.py:43
  117.6 0.7 fusion.14
  127.1 0.6 pad_maximum_fusion.2
  (3 shorter events, 0.0 us)
Async XLA Ops:
  7.2 53.5 %all-gather.2.cloned.1.call-start = ((), (), s32[]{:S(2)}) async-start(), calls=%async_computation | async-start | bytes 3899392 | tf_op jit(solution)/shard_map/all_gather | solution.py:24
  60.7 3.1 %copy-start = (bf16[2,896,1024]{2,1,0:T(8,128)(2,1)S(1)}, bf16[2,896,1024]{2,1,0:T(8,128)(2,1)}, u32[]{:S(2)}) copy-start(bf16[2,896,1024]{2,1,0:T(8,128)(2,1)} %all-gather.2.cloned.1.call-done) | copy-start | bytes 11010052
Sparse Core Ops, SparseCore 0:
  10.3 50.3 all-gather.1
where the time goes:
time: 136 us
  blocking collectives  53.8 us (40%)
  waiting for transfers between devices  36.4 us (27%)
  between operations  26 us (19%)
  other arithmetic  9.38 us (7%)
  local copies, waits for them, and re-layouts  6.55 us (5%)
  matrix products  3.5 us (3%)
    psum x1, blocking collectives, shards(): row_terms = lax.psum(row_terms, ('blk', 'grp'))  39.4 us
    all_gather x1, waiting for transfers between devices, shards(): block = lax.all_gather(stacked, 'blk', axis=1, tiled=True)  36.4 us
    all_gather x1, blocking collectives, shards(): paired = lax.all_gather(stacked, 'grp', axis=1, tiled=True)  9.49 us
    unnamed x1, blocking collectives  4.91 us
    dot_general x2, matrix products, kernel_block(): lax.dot_general(rows, cols, (((1,), (1,)), ((), ())), preferred_element_t...  3.5 us
    another operation x1, local copies, waits for them, and re-layouts, shards(): jnp.stack([jnp.sum(own_rows[0]), jnp.sum(own_rows[1]), jnp.sum(own_rows[0...  3.22 us
    reduce_sum x1, other arithmetic, kernel_block(): sq_cols = jnp.sum(cols.astype(jnp.float32) ** 2, axis=1)  2.99 us
  transfers between devices with their start and end apart: 1, of which 1 were waited for; matrix products, arithmetic and copies ran while one was open for 3% of the time, Pallas kernels for 0%

commit v1 on v0

--- a/solution.py
+++ b/solution.py
@@ -40,7 +40,8 @@
         ]
     )
     prods = lax.psum(prods, ("blk", "grp"))
-    row_terms = lax.psum(row_terms, ("blk", "grp"))
+    for over in ("grp", "blk"):
+        row_terms = lax.psum(row_terms, over)
     sum_one, sum_two = (row_terms[0], row_terms[1])
     c_cross, c_one, c_two = (row_terms[2], row_terms[3], row_terms[4])
     h_cross = prods[0] - 2.0 * c_cross / total + sum_one * sum_two / (total * total)

time: 136 us -> 170 us (1.25)
  blocking collectives: 53.8 us -> 85.6 us
    psum x1 -> x3, blocking collectives: 39.4 us -> 71.2 us  [the longest x1 36.9 us: shards(): prods = lax.psum(prods, ('blk', 'grp'))]
  transfers between devices with their start and end apart: 1 -> 1, of which waited for: 1 -> 1; matrix products, arithmetic and copies ran while one was open for 3% -> 2% of each run, Pallas kernels for 0% -> 0%
where the time goes in v1:
time: 170 us; the launch traced here: 168 us
  blocking collectives  85.6 us (50%)
  waiting for transfers between devices  36.4 us (21%)
  between operations  26.2 us (15%)
  other arithmetic  9.38 us (6%)
  local copies, waits for them, and re-layouts  7.19 us (4%)
  matrix products  3.5 us (2%)
    psum x1, blocking collectives, shards(): prods = lax.psum(prods, ('blk', 'grp'))  36.9 us
    all_gather x1, waiting for transfers between devices, shards(): block = lax.all_gather(stacked, 'blk', axis=1, tiled=True)  36.4 us
    psum x2, blocking collectives, shards(): row_terms = lax.psum(row_terms, over)  34.4 us
    all_gather x1, blocking collectives, shards(): paired = lax.all_gather(stacked, 'grp', axis=1, tiled=True)  9.49 us
    unnamed x1, blocking collectives  4.91 us
    dot_general x2, matrix products, kernel_block(): lax.dot_general(rows, cols, (((1,), (1,)), ((), ())), preferred_element_t...  3.5 us
  transfers between devices with their start and end apart: 1, of which 1 were waited for; matrix products, arithmetic and copies ran while one was open for 2% of the time, Pallas kernels for 0%

profile of v1, /device:TPU:0, one launch (start us, length us, event | category | flops | bytes accessed | tf_op | source)
XLA Modules:
  0.0 168.4 jit_solution(14954826032016480330)
XLA Ops:
  7.2 0.0 all-gather.2.cloned.1.call-start
  7.2 1.7 pad_maximum_fusion
  8.9 0.0 all-gather.2.cloned.1.call-update
  8.9 0.7 convert_element_type.14
  9.6 0.6 fusion.16
  11.5 1.2 dynamic-slice
  13.4 0.7 divide_exponential_fusion
  14.0 0.6 fusion.17
  14.6 9.5 %all_gather.6 = bf16[2,112,1024]{2,1,0:T(8,128)(2,1)S(1)} all-gather(bf16[2,56,1024]{2,1,0:T(8,128)(2,1)} %pad_maximum_fusion), channel_id=1, replica_groups=mesh['blk'=16,'grp'=2] {'grp'}, dimensions={1}, use_global_device_ids=true | all-gather | bytes 688128 | tf_op jit(solution)/shard_map/all_gather | solution.py:22
  24.1 0.2 multiply_reduce_fusion.2
  24.3 36.4 %all-gather.2.cloned.1.call-done = bf16[2,896,1024]{2,1,0:T(8,128)(2,1)} async-done(((bf16[2,56,1024]{2,1,0:T(8,128)(2,1)}), bf16[2,896,1024]{2,1,0:T(8,128)(2,1)}) %all-gather.2.cloned.1.call-update) | async-done | bytes 3670032 | tf_op jit(solution)/shard_map/all_gather | solution.py:24
  60.7 0.0 copy-start
  60.7 3.0 %multiply_reduce_fusion.1 = (f32[896]{0:T(1024)S(1)}, f32[896]{0:T(1024)S(1)}) fusion(bf16[2,896,1024]{2,1,0:T(8,128)(2,1)} %all-gather.2.cloned.1.call-done), kind=kLoop, calls=%fused_computation.1 | loop fusion | flops 5503232 | bytes 3677184 | tf_op jit(solution)/shard_map/reduce_sum | solution.py:10
  63.7 0.2 copy-done
  63.8 1.4 fusion.10
  65.2 2.1 %multiply_reduce_fusion.5 = (f32[]{:T(128)}, f32[]{:T(128)}, f32[112]{0:T(128)S(1)}, f32[]{:T(128)}, f32[112]{0:T(128)S(1)}) fusion(f32[112,896]{1,0:T(8,128)S(1)} %fusion.10, f32[]{:T(128)} %bitcast.6, f32[]{:T(128)} %bitcast.5, bf16[2,896,1024]{2,1,0:T(8,128)(2,1)S(1)} %copy-done, bf16[2,112,1024]{2,1,0:T(8,128)(2,1)S(1)} %all_gather.6, ...), kind=kOutput, calls=%fused_computation.21 | convolution fusion | flops 206925600 | bytes 2471316 | tf_op jit(solution)/shard_map/dot_general | solution.py:11
  67.4 4.9 %all-reduce = f32[2,112]{1,0:T(2,128)S(1)} all-reduce(f32[2,112]{1,0:T(2,128)S(1)} %pad_maximum_fusion.1), channel_id=2, replica_groups=mesh['blk'=16,'grp'=2] {'grp'}, use_global_device_ids=true, to_apply=%region_5.0.clone | all-reduce | flops 224 | bytes 1792
  72.3 0.1 constant_dynamic-slice_fusion
  72.4 0.7 multiply_reduce_fusion.6
  73.0 3.2 %stack.64 = f32[5]{0:T(128)S(1)} concatenate(f32[1]{0:T(128)} %bitcast.14, f32[1]{0:T(128)} %bitcast.15, f32[1]{0:T(128)} %bitcast.16, f32[1]{0:T(128)} %bitcast.17, f32[1]{0:T(128)} %bitcast.18), dimensions={0} | concatenate | bytes 40 | tf_op jit(solution)/shard_map/stack | solution.py:33
  76.2 4.9 %psum.21 = f32[5]{0:T(128)S(1)} all-reduce(f32[5]{0:T(128)S(1)} %stack.64), channel_id=1, replica_groups=mesh['blk'=16,'grp'=2] {'grp'}, use_global_device_ids=true, to_apply=%region_11.0 | all-reduce | flops 5 | bytes 40 | tf_op jit(solution)/shard_map/psum | solution.py:44
  81.2 29.5 %psum.22 = f32[5]{0:T(128)S(1)} all-reduce(f32[5]{0:T(128)S(1)} %psum.21), channel_id=1, replica_groups=mesh['blk'=16,'grp'=2] {'blk'}, use_global_device_ids=true, to_apply=%region_12.0 | all-reduce | flops 5 | bytes 40 | tf_op jit(solution)/shard_map/psum | solution.py:44
  110.6 0.6 fusion.15
  116.9 2.0 %pad_maximum_fusion.3 = f32[3]{0:T(128)S(1)} fusion(f32[1]{0:T(128)} %bitcast.23, f32[1]{0:T(128)} %bitcast.22, f32[1]{0:T(128)} %bitcast.21), kind=kLoop, calls=%fused_computation.27 | loop fusion | flops 6 | bytes 24 | tf_op jit(solution)/shard_map/stack | solution.py:29
  119.5 36.9 %psum.23 = f32[3]{0:T(128)S(1)} all-reduce(f32[3]{0:T(128)S(1)} %pad_maximum_fusion.3), channel_id=1, replica_groups=mesh['blk'=16,'grp'=2] {'blk','grp'}, use_global_device_ids=true, to_apply=%region_16.0 | all-reduce | flops 3 | bytes 24 | tf_op jit(solution)/shard_map/psum | solution.py:42
  156.4 0.7 fusion.14
  159.8 0.6 pad_maximum_fusion.2
  (3 shorter events, 0.0 us)
Async XLA Ops:
  7.2 53.5 %all-gather.2.cloned.1.call-start = ((), (), s32[]{:S(2)}) async-start(), calls=%async_computation | async-start | bytes 3899392 | tf_op jit(solution)/shard_map/all_gather | solution.py:24
  60.7 3.1 %copy-start = (bf16[2,896,1024]{2,1,0:T(8,128)(2,1)S(1)}, bf16[2,896,1024]{2,1,0:T(8,128)(2,1)}, u32[]{:S(2)}) copy-start(bf16[2,896,1024]{2,1,0:T(8,128)(2,1)} %all-gather.2.cloned.1.call-done) | copy-start | bytes 11010052
Sparse Core Ops, SparseCore 0:
  10.3 50.3 all-gather.1
